TPU v7x, 128 devices: a whole 4x4x4 slice. The times are simulated.
128 devices in a mesh: seq: 8 (over y_lo, x), tp: 8 (over z, core), grp: 2 (over y_hi).
Axes of the slice: x: 4, y: 4 (y_hi: 2, y_lo: 2; y = y_hi * 2 + y_lo), z: 4, core: 2. Of those that a mesh axis runs over, the one named last changes fastest.
Arguments:
- query: bfloat16 [16, 64, 8192], P('grp', None, 'tp'), parts along dimension 0, may hold values from -15 to 15
- cache: bfloat16 [16, 16384, 8, 256], P('grp', 'tp', 'seq'), parts along dimension 0, may hold values from -6 to 6
- head_of_slot: int32 [16], P('grp'), parts along dimension 0, may hold values from 0 to 7, each once
- lengths: int32 [16], P('grp'), parts along dimension 0, may hold values from 8192 to 16384
- out_weight: bfloat16 [8192, 8192], P('tp', 'seq'), may hold values from -0.0625 to 0.0625
Outputs:
- projected: bfloat16 [16, 64, 8192], P(('grp', 'tp'), None, 'seq'), parts along dimension 0
There are 2 independent parts, one for each index of `grp`. A program takes and returns all parts, laid end to end along the dimension named above; an argument that names none is the same for every part. Nothing has to cross between parts.
Inputs may be any that keep to these rules, and one draw needn't show every extreme that they name: head_of_slot names every KV head exactly once.
All inputs are finite; a program needn't handle non-finite values.
Results may differ from a plain program's by a relative error of at most 0.01.
Values may be sent and summed in bfloat16 or wider, within the bound.
A program may use at most 128 MiB of HBM per device.

v0:
```python
import math

import jax
import jax.numpy as jnp
from jax import lax
from jax.sharding import PartitionSpec as P

HQ = 64
KVH = 8


MASKED_SCORE = -1e30


def from_root(shard, axis, root):
    return lax.dynamic_index_in_dim(lax.all_gather(shard, axis), root, 0, keepdims=False)


def merged(shard, axis, combine):
    everything = jax.tree.map(lambda part: lax.all_gather(part, axis), shard)
    first = jax.tree.map(lambda part: part[0], everything)

    def step(k, so_far):
        return combine(so_far, jax.tree.map(lambda part: part[k], everything))

    return lax.fori_loop(1, lax.axis_size(axis), step, first)


def split_up(shard, dim, length):
    before, after = (shard.shape[:dim], shard.shape[dim + 1 :])
    return jnp.moveaxis(shard.reshape(*before, length, -1, *after), dim, 0)


def sum_at_owner(shard, axis, dim):
    pieces = split_up(shard, dim, lax.axis_size(axis))
    arrived = lax.all_to_all(pieces, axis, split_axis=0, concat_axis=0, tiled=True)
    return arrived.sum(axis=0)


def slot_table(head_of_slot):
    slot_total = head_of_slot.shape[0]
    slot_ids = jnp.arange(slot_total, dtype=jnp.int32)
    return jnp.sum(
        jnp.where(head_of_slot[None, :] == slot_ids[:, None], slot_ids[None, :], 0), axis=1
    )


def combine(earlier, latter):
    maxima = jnp.maximum(earlier[0], latter[0])
    early_scale = jnp.exp(earlier[0] - maxima)
    late_scale = jnp.exp(latter[0] - maxima)
    totals = earlier[1] * early_scale + latter[1] * late_scale
    blended = earlier[2] * early_scale[..., None] + latter[2] * late_scale[..., None]
    return (maxima, totals, blended)


def partial_attention(queries, entries, positions, lengths, group_size):
    seq_total, tokens = (queries.shape[0], queries.shape[1])
    head_count = entries.shape[2]
    head_dim = entries.shape[3] // 2
    row_count = tokens * group_size
    stacked = queries.reshape(seq_total, tokens, head_count, group_size, head_dim)
    stacked = stacked.transpose(0, 2, 1, 3, 4).reshape(seq_total, head_count, row_count, head_dim)
    limits = (
        lengths[:, None] - tokens + jnp.arange(row_count, dtype=jnp.int32)[None, :] // group_size
    )
    scaling = 1.0 / math.sqrt(head_dim)
    extent = entries.shape[1]
    block_len = math.gcd(extent, 512)

    def advance(turn_index, carried):
        maxima, totals, blended = carried
        first_pos = turn_index * block_len
        entry_block = lax.dynamic_slice_in_dim(entries, first_pos, block_len, 1)
        block_pos = lax.dynamic_slice_in_dim(positions, first_pos, block_len, 0)
        scores = (
            jnp.einsum(
                "bnrd,bknd->bnrk",
                stacked,
                entry_block[..., :head_dim],
                preferred_element_type=jnp.float32,
            )
            * scaling
        )
        visible = block_pos[None, None, None, :] <= limits[:, None, :, None]
        scores = jnp.where(visible, scores, MASKED_SCORE)
        new_max = jnp.maximum(maxima, jnp.max(scores, axis=3))
        shrink = jnp.exp(maxima - new_max)
        weights = jnp.where(visible, jnp.exp(scores - new_max[..., None]), 0.0)
        totals = totals * shrink + jnp.sum(weights, axis=3)
        blended = blended * shrink[..., None] + jnp.einsum(
            "bnrk,bknd->bnrd",
            weights.astype(jnp.bfloat16),
            entry_block[..., head_dim:],
            preferred_element_type=jnp.float32,
        )
        return (new_max, totals, blended)

    initial = (
        jnp.full((seq_total, head_count, row_count), MASKED_SCORE, jnp.float32),
        jnp.zeros((seq_total, head_count, row_count), jnp.float32),
        jnp.zeros((seq_total, head_count, row_count, head_dim), jnp.float32),
    )
    return lax.fori_loop(0, extent // block_len, advance, initial)


def normalize(totals, blended, tokens, group_size):
    seq_total, head_count, row_count, head_dim = blended.shape
    attended = (blended / totals[..., None]).astype(jnp.bfloat16)
    attended = attended.reshape(seq_total, head_count, tokens, group_size, head_dim).transpose(
        0, 2, 1, 3, 4
    )
    return attended.reshape(seq_total, tokens, head_count * group_size * head_dim)


def local(query, cache, head_of_slot, lengths, out_weight):
    group_size = HQ // KVH
    seq_devices = lax.axis_size("seq")
    tp_devices = lax.axis_size("tp")
    seq_rank = lax.axis_index("seq")
    tp_rank = lax.axis_index("tp")
    slot_of_head = slot_table(head_of_slot)
    seq_total, tokens = (query.shape[0], query.shape[1])
    per_seq = KVH // seq_devices
    per_tp = KVH // tp_devices
    offset = 0
    kv_head = head_of_slot[seq_rank * per_seq + offset]
    received = from_root(query, "tp", kv_head // per_tp)
    fetched = received
    extent = cache.shape[1]
    positions = tp_rank * extent + jnp.arange(extent, dtype=jnp.int32)
    partials = partial_attention(fetched, cache, positions, lengths, group_size)
    maxima, totals, blended = merged(partials, "tp", combine)
    by_slot = normalize(totals, blended, tokens, group_size)
    offset = 0
    slot_index = slot_of_head[tp_rank * per_tp + offset]
    received = from_root(by_slot, "seq", slot_index // per_seq)
    flattened = received.reshape(seq_total * tokens, received.shape[2])
    summed = sum_at_owner(
        jnp.dot(flattened, out_weight, preferred_element_type=jnp.float32), "tp", 0
    )
    return summed.astype(jnp.bfloat16).reshape(seq_total // tp_devices, tokens, summed.shape[1])


def solution(mesh):
    in_specs = (
        P("grp", None, "tp"),
        P("grp", "tp", "seq", None),
        P("grp"),
        P("grp"),
        P("tp", "seq"),
    )
    out_specs = P(("grp", "tp"), None, "seq")
    return jax.shard_map(local, mesh=mesh, in_specs=in_specs, out_specs=out_specs, check_vma=False)
```

profile of v0, /device:TPU:1, one launch (start us, length us, event | category | flops | bytes accessed | tf_op | source)
XLA Modules:
  0.0 367.1 jit_solution(11894439987226109700)
XLA Ops:
  11.4 51.2 %all-gather.10.cloned.1.call-done = bf16[64,64,1024]{2,1,0:T(8,128)(2,1)} async-done(((bf16[8,64,1024]{2,1,0:T(8,128)(2,1)}), bf16[64,64,1024]{2,1,0:T(8,128)(2,1)}) %all-gather.10.cloned.1.call-update) | async-done | bytes 8388624 | tf_op jit(solution)/shard_map/all_gather | solution.py:16
  65.2 47.7 %while.38 = (s32[]{:T(128)}, f32[8,1,512]{2,0,1:T(8,128)S(1)}, f32[8,1,512]{2,0,1:T(8,128)S(1)}, f32[8,1,512,128]{3,2,0,1:T(8,128)}, s32[2048]{0:T(1024)S(1)}, /...) while((s32[]{:T(128)}, f32[8,1,512]{2,0,1:T(8,128)S(1)}, ...), condition=%wide.region_3.4_spmd.clone, body=%wide.region_0.3_spmd.clone.sunk | while | flops 1108897792 | bytes 49623352 | solution.py:104
  65.3 3.0 fusion.39
  70.9 4.9 %bitcast_add_fusion.5 = f32[8,1,512,128]{3,2,0,1:T(8,128)S(1)} fusion(f32[8,1,512,128]{3,2,0,1:T(8,128)S(1)} %copy-done.1, f32[8,512,512]{2,1,0:T(8,128)S(1)} %get-tuple-element.568, f32[8,512]{1,0:T(8,128)S(1)} %bitcast.116, s32[8,512]{1,0:T(8,128)S(1)} %broadcast_add_fusion.3, s32[512]{0:T(512)S(1)} %dynamic_slice.76, ...), kind=kOutput, calls=%fused_computation.20.clone.1 | convolution fusion | flops 551026688 | bytes 13682697 | tf_op jit(solution)/shard_map/while/body/eval_jaxpr/bnrk,bknd->bnrd/dot_general | solution.py:91
  77.2 3.0 fusion.39
  82.8 4.9 %bitcast_add_fusion.5 = f32[8,1,512,128]{3,2,0,1:T(8,128)S(1)} fusion(f32[8,1,512,128]{3,2,0,1:T(8,128)S(1)} %copy-done.1, f32[8,512,512]{2,1,0:T(8,128)S(1)} %get-tuple-element.568, f32[8,512]{1,0:T(8,128)S(1)} %bitcast.116, s32[8,512]{1,0:T(8,128)S(1)} %broadcast_add_fusion.3, s32[512]{0:T(512)S(1)} %dynamic_slice.76, ...), kind=kOutput, calls=%fused_computation.20.clone.1 | convolution fusion | flops 551026688 | bytes 13682697 | tf_op jit(solution)/shard_map/while/body/eval_jaxpr/bnrk,bknd->bnrd/dot_general | solution.py:91
  89.2 3.0 fusion.39
  94.7 4.9 %bitcast_add_fusion.5 = f32[8,1,512,128]{3,2,0,1:T(8,128)S(1)} fusion(f32[8,1,512,128]{3,2,0,1:T(8,128)S(1)} %copy-done.1, f32[8,512,512]{2,1,0:T(8,128)S(1)} %get-tuple-element.568, f32[8,512]{1,0:T(8,128)S(1)} %bitcast.116, s32[8,512]{1,0:T(8,128)S(1)} %broadcast_add_fusion.3, s32[512]{0:T(512)S(1)} %dynamic_slice.76, ...), kind=kOutput, calls=%fused_computation.20.clone.1 | convolution fusion | flops 551026688 | bytes 13682697 | tf_op jit(solution)/shard_map/while/body/eval_jaxpr/bnrk,bknd->bnrd/dot_general | solution.py:91
  101.1 3.0 fusion.39
  106.6 4.9 %bitcast_add_fusion.5 = f32[8,1,512,128]{3,2,0,1:T(8,128)S(1)} fusion(f32[8,1,512,128]{3,2,0,1:T(8,128)S(1)} %copy-done.1, f32[8,512,512]{2,1,0:T(8,128)S(1)} %get-tuple-element.568, f32[8,512]{1,0:T(8,128)S(1)} %bitcast.116, s32[8,512]{1,0:T(8,128)S(1)} %broadcast_add_fusion.3, s32[512]{0:T(512)S(1)} %dynamic_slice.76, ...), kind=kOutput, calls=%fused_computation.20.clone.1 | convolution fusion | flops 551026688 | bytes 13682697 | tf_op jit(solution)/shard_map/while/body/eval_jaxpr/bnrk,bknd->bnrd/dot_general | solution.py:91
  112.9 12.9 %all-gather.1 = f32[64,1,512]{2,0,1:T(8,128)S(1)} all-gather(f32[8,1,512]{2,0,1:T(8,128)S(1)} %get-tuple-element.323), channel_id=3, replica_groups=mesh['seq'=8,'tp'=8,'grp'=2] {'tp'}, dimensions={0}, use_global_device_ids=true | all-gather | bytes 147456 | tf_op jit(solution)/shard_map/all_gather | solution.py:20
  125.8 13.3 %all-gather.2 = f32[64,1,512]{2,0,1:T(8,128)S(1)} all-gather(f32[8,1,512]{2,0,1:T(8,128)S(1)} %get-tuple-element.324), channel_id=4, replica_groups=mesh['seq'=8,'tp'=8,'grp'=2] {'tp'}, dimensions={0}, use_global_device_ids=true | all-gather | bytes 147456 | tf_op jit(solution)/shard_map/all_gather | solution.py:20
  139.2 59.5 %all-gather.12.cloned.1.call-done = f32[64,1,512,128]{3,2,1,0:T(8,128)} async-done(((f32[8,1,512,128]{3,2,1,0:T(8,128)}), f32[64,1,512,128]{3,2,1,0:T(8,128)}) %all-gather.12.cloned.1.call-update) | async-done | bytes 16777232 | tf_op jit(solution)/shard_map/all_gather | solution.py:20
  198.7 3.1 slice.33
  201.8 27.4 %while.37 = (s32[]{:T(128)}, f32[8,1,512]{2,1,0:T(1,128)S(1)}, f32[8,1,512]{2,1,0:T(1,128)S(1)}, f32[8,1,512,128]{3,2,1,0:T(8,128)}, f32[8,8,1,512]{3,1,0,2:T(8,...) while((s32[]{:T(128)}, f32[8,1,512]{2,1,0:T(1,128)S(1)}, ...), condition=%wide.region_5.6_spmd, body=%wide.region_4.5_spmd.sunk | while | flops 1597445 | bytes 6586511 | solution.py:26
  201.9 3.8 %fusion.37 = f32[8,1,512,128]{3,2,1,0:T(8,128)} fusion(f32[8,8,1,512,128]{4,3,1,2,0:T(8,128)} %get-tuple-element.638, s32[]{:T(128)S(6)} %select_n.106, f32[8,1,512,128]{3,2,1,0:T(8,128)} %get-tuple-element.625, f32[8,512]{1,0:T(8,128)S(1)} %bitcast.118, f32[8,512]{1,0:T(8,128)S(1)} %bitcast.119), kind=kLoop, calls=%fused_computation.2.clone.1 | loop fusion | flops 1572864 | bytes 6324228 | tf_op jit(solution)/shard_map/while/body/eval_jaxpr/add | solution.py:53
  205.8 3.8 %fusion.37 = f32[8,1,512,128]{3,2,1,0:T(8,128)} fusion(f32[8,8,1,512,128]{4,3,1,2,0:T(8,128)} %get-tuple-element.638, s32[]{:T(128)S(6)} %select_n.106, f32[8,1,512,128]{3,2,1,0:T(8,128)} %get-tuple-element.625, f32[8,512]{1,0:T(8,128)S(1)} %bitcast.118, f32[8,512]{1,0:T(8,128)S(1)} %bitcast.119), kind=kLoop, calls=%fused_computation.2.clone.1 | loop fusion | flops 1572864 | bytes 6324228 | tf_op jit(solution)/shard_map/while/body/eval_jaxpr/add | solution.py:53
  209.8 3.8 %fusion.37 = f32[8,1,512,128]{3,2,1,0:T(8,128)} fusion(f32[8,8,1,512,128]{4,3,1,2,0:T(8,128)} %get-tuple-element.638, s32[]{:T(128)S(6)} %select_n.106, f32[8,1,512,128]{3,2,1,0:T(8,128)} %get-tuple-element.625, f32[8,512]{1,0:T(8,128)S(1)} %bitcast.118, f32[8,512]{1,0:T(8,128)S(1)} %bitcast.119), kind=kLoop, calls=%fused_computation.2.clone.1 | loop fusion | flops 1572864 | bytes 6324228 | tf_op jit(solution)/shard_map/while/body/eval_jaxpr/add | solution.py:53
  213.7 3.8 %fusion.37 = f32[8,1,512,128]{3,2,1,0:T(8,128)} fusion(f32[8,8,1,512,128]{4,3,1,2,0:T(8,128)} %get-tuple-element.638, s32[]{:T(128)S(6)} %select_n.106, f32[8,1,512,128]{3,2,1,0:T(8,128)} %get-tuple-element.625, f32[8,512]{1,0:T(8,128)S(1)} %bitcast.118, f32[8,512]{1,0:T(8,128)S(1)} %bitcast.119), kind=kLoop, calls=%fused_computation.2.clone.1 | loop fusion | flops 1572864 | bytes 6324228 | tf_op jit(solution)/shard_map/while/body/eval_jaxpr/add | solution.py:53
  217.6 3.8 %fusion.37 = f32[8,1,512,128]{3,2,1,0:T(8,128)} fusion(f32[8,8,1,512,128]{4,3,1,2,0:T(8,128)} %get-tuple-element.638, s32[]{:T(128)S(6)} %select_n.106, f32[8,1,512,128]{3,2,1,0:T(8,128)} %get-tuple-element.625, f32[8,512]{1,0:T(8,128)S(1)} %bitcast.118, f32[8,512]{1,0:T(8,128)S(1)} %bitcast.119), kind=kLoop, calls=%fused_computation.2.clone.1 | loop fusion | flops 1572864 | bytes 6324228 | tf_op jit(solution)/shard_map/while/body/eval_jaxpr/add | solution.py:53
  221.5 3.8 %fusion.37 = f32[8,1,512,128]{3,2,1,0:T(8,128)} fusion(f32[8,8,1,512,128]{4,3,1,2,0:T(8,128)} %get-tuple-element.638, s32[]{:T(128)S(6)} %select_n.106, f32[8,1,512,128]{3,2,1,0:T(8,128)} %get-tuple-element.625, f32[8,512]{1,0:T(8,128)S(1)} %bitcast.118, f32[8,512]{1,0:T(8,128)S(1)} %bitcast.119), kind=kLoop, calls=%fused_computation.2.clone.1 | loop fusion | flops 1572864 | bytes 6324228 | tf_op jit(solution)/shard_map/while/body/eval_jaxpr/add | solution.py:53
  225.4 3.8 %fusion.37 = f32[8,1,512,128]{3,2,1,0:T(8,128)} fusion(f32[8,8,1,512,128]{4,3,1,2,0:T(8,128)} %get-tuple-element.638, s32[]{:T(128)S(6)} %select_n.106, f32[8,1,512,128]{3,2,1,0:T(8,128)} %get-tuple-element.625, f32[8,512]{1,0:T(8,128)S(1)} %bitcast.118, f32[8,512]{1,0:T(8,128)S(1)} %bitcast.119), kind=kLoop, calls=%fused_computation.2.clone.1 | loop fusion | flops 1572864 | bytes 6324228 | tf_op jit(solution)/shard_map/while/body/eval_jaxpr/add | solution.py:53
  235.2 89.2 %all-gather.8.cloned.1.call-done = bf16[8,8,64,1024]{3,2,1,0:T(8,128)(2,1)} async-done(((bf16[1,8,64,1024]{3,2,1,0:T(8,128)(2,1)}), bf16[8,8,64,1024]{3,2,1,0:T(8,128)(2,1)}) %all-gather.8.cloned.1.call-update) | async-done | bytes 8388624 | tf_op jit(solution)/shard_map/all_gather | solution.py:16
  326.9 31.3 %all_to_all.5 = f32[8,64,1024]{2,1,0:T(8,128)} all-to-all(f32[8,64,1024]{2,1,0:T(8,128)S(1)} %fusion.21), channel_id=1, replica_groups=mesh['seq'=8,'tp'=8,'grp'=2] {'tp'}, dimensions={0} | all-to-all | bytes 4194304 | tf_op jit(solution)/shard_map/all_to_all | solution.py:36
  (98 shorter events, 30.8 us)
Async XLA Ops:
  6.5 317.8 %copy-start = (bf16[1024,1024]{1,0:T(8,128)(2,1)S(1)}, bf16[1024,1024]{1,0:T(8,128)(2,1)}, u32[]{:S(2)}) copy-start(bf16[1024,1024]{1,0:T(8,128)(2,1)} %param.13) | copy-start | bytes 6291460
  6.5 56.0 %all-gather.10.cloned.1.call-start = ((), (), s32[]{:S(2)}) async-start(), calls=%async_computation.2 | async-start | bytes 9437184 | tf_op jit(solution)/shard_map/all_gather | solution.py:16
  7.3 191.5 %all-gather.12.cloned.1.call-start = ((), (), s32[]{:S(2)}) async-start(), calls=%async_computation.3 | async-start | bytes 18874368 | tf_op jit(solution)/shard_map/all_gather | solution.py:20
  65.3 5.5 %copy-start.1 = (f32[8,1,512,128]{3,2,0,1:T(8,128)S(1)}, f32[8,1,512,128]{3,2,0,1:T(8,128)}, u32[]{:S(2)}) copy-start(f32[8,1,512,128]{3,2,0,1:T(8,128)} %get-tuple-element.587) | copy-start | bytes 6291460 | tf_op jit(solution)/shard_map/while
  75.8 1.3 copy-start.2
  77.2 5.5 %copy-start.1 = (f32[8,1,512,128]{3,2,0,1:T(8,128)S(1)}, f32[8,1,512,128]{3,2,0,1:T(8,128)}, u32[]{:S(2)}) copy-start(f32[8,1,512,128]{3,2,0,1:T(8,128)} %get-tuple-element.587) | copy-start | bytes 6291460 | tf_op jit(solution)/shard_map/while
  87.7 1.3 copy-start.2
  89.2 5.5 %copy-start.1 = (f32[8,1,512,128]{3,2,0,1:T(8,128)S(1)}, f32[8,1,512,128]{3,2,0,1:T(8,128)}, u32[]{:S(2)}) copy-start(f32[8,1,512,128]{3,2,0,1:T(8,128)} %get-tuple-element.587) | copy-start | bytes 6291460 | tf_op jit(solution)/shard_map/while
  99.6 1.3 copy-start.2
  101.1 5.5 %copy-start.1 = (f32[8,1,512,128]{3,2,0,1:T(8,128)S(1)}, f32[8,1,512,128]{3,2,0,1:T(8,128)}, u32[]{:S(2)}) copy-start(f32[8,1,512,128]{3,2,0,1:T(8,128)} %get-tuple-element.587) | copy-start | bytes 6291460 | tf_op jit(solution)/shard_map/while
  111.5 1.3 copy-start.2
  112.9 211.5 %all-gather.8.cloned.1.call-start = ((), (), s32[]{:S(2)}) async-start(), calls=%async_computation.1 | async-start | bytes 9437184 | tf_op jit(solution)/shard_map/all_gather | solution.py:16
  201.8 30.7 %copy-start.3 = (s32[8]{0:T(128)S(1)}, s32[8]{0:T(128)}, u32[]{:S(2)}) copy-start(s32[8]{0:T(128)} %param.11) | copy-start | bytes 100
Sparse Core Ops, SparseCore 0:
  9.0 53.4 all-gather.9
  113.0 85.6 all-gather.11
  232.7 91.6 all-gather.7
where the time goes:
time: 368 us; the launch traced here: 367 us
  waiting for transfers between devices  201 us (55%)
  blocking collectives  57.5 us (16%)
  other arithmetic  42.7 us (12%)
  matrix products  34.1 us (9%)
  between operations  17.2 us (5%)
  local copies, waits for them, and re-layouts  14.6 us (4%)
    all_gather x2, waiting for transfers between devices, from_root(): lax.all_gather(shard, axis)  140 us
    all_gather x1, waiting for transfers between devices, merged(): everything = jax.tree.map(lambda part: lax.all_gather(part, axis), shard)  59.5 us
    all_to_all x1, blocking collectives, sum_at_owner(): lax.all_to_all(pieces, axis, split_axis=0, concat_axis=0, tiled=True)  31.3 us
    add x7, other arithmetic, combine(): earlier[2] * early_scale[..., None] + latter[2] * late_scale[..., None]  26.7 us
    all_gather x2, blocking collectives, merged(): everything = jax.tree.map(lambda part: lax.all_gather(part, axis), shard)  26.2 us
    dot_general x4, matrix products, advance(): jnp.einsum('bnrk,bknd->bnrd', weights.astype(jnp.bfloat16), entry_block[....  19.5 us
    dot_general x4, matrix products, advance(): jnp.einsum('bnrd,bknd->bnrk', stacked, entry_block[..., :head_dim], prefe...  12.1 us
    reduce_sum x4, other arithmetic, advance(): totals = totals * shrink + jnp.sum(weights, axis=3)  9.91 us
  transfers between devices with their start and end apart: 3, of which 3 were waited for; matrix products, arithmetic and copies ran while one was open for 1% of the time, Pallas kernels for 0%

commit v1 on v0

v1 whole, which is shorter than its diff:
```python
import functools
import math

import jax
import jax.numpy as jnp
from jax import lax
from jax.experimental import pallas as pl
from jax.experimental.pallas import tpu as pltpu
from jax.sharding import PartitionSpec as P

HQ = 64
KVH = 8
HD = 128
NB = 8
QT = 64
GS = 8
ROWS = GS * QT
TILE = 256
MASKED = -1e30
EXP2_SCALE = math.log2(math.e) / math.sqrt(HD)
F32 = jnp.float32
BF16 = jnp.bfloat16
MESH = pl.DeviceIdType.MESH
Q0, Q1, Q2, Q3, ML, C1, C2, C3, C4 = range(9)
NCH = 4


def kernel(
    heads_ref, len_ref, q_hbm, kv_hbm, w_hbm, out_ref,
    qown, q0recv, cand, q1recv, qall, kv, w, kx, s0, s1, p0, p1, ms0, ms1,
    oacc, mlbuf, mlrecv, osend, c1recv, c2send, c2recv, psum, c3recv, attall,
    ybuf, d1recv, d2send, d2recv, ssem, rsem, dssem, drsem, lsem,
):
    s = lax.axis_index("seq")
    t = lax.axis_index("tp")
    z = t // 2
    c = t % 2
    other = 1 - c
    length = kv.shape[1]
    head = heads_ref[s]
    head_chip = head // 2
    head_core = head % 2

    def slot_of(h):
        slot = jnp.int32(0)
        for k in range(KVH):
            slot = jnp.where(heads_ref[k] == h, k, slot)
        return slot

    my_slots = [slot_of(2 * k + c) for k in range(4)]
    other_slots = [slot_of(2 * k + other) for k in range(4)]

    partner = {"tp": t + 1 - 2 * c}

    def zpeer(d):
        zz = (z + d) % 4
        return zz, {"tp": 2 * zz + c}

    def send(src, dst, ss, rs, dev):
        pltpu.make_async_remote_copy(
            src_ref=src, dst_ref=dst, send_sem=ss, recv_sem=rs, device_id=dev, device_id_type=MESH
        ).start()

    def got(ref, rs):
        pltpu.make_async_remote_copy(
            src_ref=ref, dst_ref=ref, send_sem=rs, recv_sem=rs, device_id=partner, device_id_type=MESH
        ).wait_recv()

    def sent(ref, ss):
        pltpu.make_async_remote_copy(
            src_ref=ref, dst_ref=ref, send_sem=ss, recv_sem=ss, device_id=partner, device_id_type=MESH
        ).wait_send()

    qload = pltpu.make_async_copy(q_hbm, qown, lsem.at[NB])
    qload.start()

    def kv_load(b):
        return pltpu.make_async_copy(kv_hbm.at[b], kv.at[b], lsem.at[b])

    wload = pltpu.make_async_copy(w_hbm, w, lsem.at[NB + 1])
    for b in range(NB):
        kv_load(b).start()
    wload.start()

    barrier = pltpu.get_barrier_semaphore()
    for d in range(1, 8):
        pl.semaphore_signal(barrier, inc=1, device_id={"tp": (t + d) % 8}, device_id_type=MESH)
        pl.semaphore_signal(barrier, inc=1, device_id={"seq": (s + d) % 8}, device_id_type=MESH)

    p1[...] = jnp.zeros_like(p1)
    qload.wait()
    pl.semaphore_wait(barrier, 14)

    half = pl.multiple_of(c * 512, 512)
    other_half = pl.multiple_of(other * 512, 512)
    for b in range(NB):
        send(qown.at[b, :, pl.ds(other_half, 512)], q0recv.at[b], ssem.at[Q0, b], rsem.at[Q0, b], partner)

    def q1(b):
        got(q0recv.at[b], rsem.at[Q0, b])
        mine = qown[b, :, pl.ds(half, 512)]
        x = jnp.where(head_core == c, mine, q0recv[b])
        for k in range(4):
            cand[b, k] = x[:, k * HD : (k + 1) * HD]
        q1recv[b, z] = cand[b, z]
        for d in (1, 3, 2):
            zz, dev = zpeer(d)
            send(cand.at[b, zz], q1recv.at[b, z], ssem.at[Q1, b], rsem.at[Q1, b], dev)

    def q2(b):
        got(q1recv.at[b, pl.ds(0, 3)], rsem.at[Q1, b])
        x = q1recv[b, 0]
        for k in range(1, 4):
            x = jnp.where(head_chip == k, q1recv[b, k], x)
        qall[b, 4 * c + z] = x
        for d in (1, 3, 2):
            _, dev = zpeer(d)
            piece = qall.at[b, 4 * c + z]
            send(piece, piece, ssem.at[Q2, b], rsem.at[Q2, b], dev)

    def q3(b):
        got(q1recv.at[b, pl.ds(0, 3)], rsem.at[Q2, b])
        piece = qall.at[b, pl.ds(4 * c, 4)]
        send(piece, piece, ssem.at[Q3, b], rsem.at[Q3, b], partner)

    def q4(b):
        got(qall.at[b, pl.ds(4 * other, 4)], rsem.at[Q3, b])

    S, PR, M = (s0, s1), (p0, p1), (ms0, ms1)
    row_of = lax.broadcasted_iota(jnp.int32, (TILE, HD), 0)
    lane_of = lax.broadcasted_iota(jnp.int32, (TILE, HD), 1)
    hot = jnp.where(row_of % QT == lane_of, 1.0, 0.0).astype(BF16)
    diag = row_of[:HD] == lane_of[:HD]

    def to_lanes(x):
        return jnp.sum(jnp.where(diag, x, 0.0), axis=0, keepdims=True)

    def to_rows(x):
        return jnp.sum(jnp.where(diag, jnp.broadcast_to(x, (HD, HD)), 0.0), axis=1, keepdims=True)

    def make_bias(b):
        start = t * length - (len_ref[b] - QT)
        pos = lax.broadcasted_iota(jnp.int32, (length, HD), 0) + start
        col = lax.broadcasted_iota(jnp.int32, (length, HD), 1)
        kx[...] = jnp.where(pos > col, MASKED, 0.0).astype(BF16)

    def qk(b, r):
        q = jnp.concatenate([qall[b, pl.ds(4 * r, 4)].reshape(TILE, HD), hot], axis=1)
        top = None
        for k in range(length // 512):
            keys = jnp.concatenate([kv[b, k * 512 : (k + 1) * 512, :HD], kx[k * 512 : (k + 1) * 512, :]], axis=1)
            x = lax.dot_general(q, keys, (((1,), (1,)), ((), ())), preferred_element_type=F32)
            S[r][:, k * 512 : (k + 1) * 512] = x
            for j in range(4):
                part = x[:, j * HD : (j + 1) * HD]
                top = part if top is None else jnp.maximum(top, part)
        m = jnp.broadcast_to(jnp.max(top, axis=1, keepdims=True), (TILE, HD))
        M[r][...] = m
        for u in range(2):
            mlbuf[b, 2 * r + u : 2 * r + u + 1, :] = to_lanes(m[u * HD : (u + 1) * HD])

    def weigh(r):
        m = M[r][...]
        for k in range(length // HD):
            x = S[r][:, k * HD : (k + 1) * HD]
            PR[r][:, k * HD : (k + 1) * HD] = jnp.exp2((x - m) * EXP2_SCALE).astype(BF16)

    def pv(b, r):
        vals = jnp.concatenate([kv[b, :, HD:], jnp.ones((length, HD), BF16)], axis=1)
        acc = jnp.dot(PR[r][...], vals, preferred_element_type=F32)
        oacc[b, r * TILE : (r + 1) * TILE, :] = acc[:, :HD]
        for u in range(2):
            mlbuf[b, 4 + 2 * r + u : 5 + 2 * r + u, :] = to_lanes(acc[u * HD : (u + 1) * HD, HD:])

    def ml(b):
        mlrecv[b, t] = mlbuf[b]
        for d in range(1, 8):
            send(mlbuf.at[b], mlrecv.at[b, t], ssem.at[ML, b], rsem.at[ML, b], {"tp": (t + d) % 8})

    def c1(b):
        got(mlrecv.at[b, pl.ds(0, 7)], rsem.at[ML, b])
        every = mlrecv[b]
        maxima = every[:, :4, :]
        top = jnp.max(maxima, axis=0)
        total = jnp.sum(every[:, 4:, :] * jnp.exp2((maxima - top[None]) * EXP2_SCALE), axis=0)
        scale = jnp.exp2((mlbuf[b, :4, :] - top) * EXP2_SCALE) / total
        for u in range(4):
            o = oacc[b, u * HD : (u + 1) * HD, :] * to_rows(scale[u : u + 1])
            osend[b, 2 * u : 2 * u + 2] = o.astype(BF16).reshape(2, QT, HD)
        c1recv[b, s] = osend[b, s]
        for d in range(1, 8):
            ss = (s + d) % 8
            send(osend.at[b, ss], c1recv.at[b, s], ssem.at[C1, b], rsem.at[C1, b], {"seq": ss})

    def pick(pieces, index):
        x = pieces[0]
        for k in range(1, len(pieces)):
            x = jnp.where(index == k, pieces[k], x)
        return x

    def c2(b):
        got(c1recv.at[b, pl.ds(0, 7)], rsem.at[C1, b])
        pieces = [c1recv[b, k] for k in range(KVH)]
        for k in range(4):
            c2send[b, k] = pick(pieces, other_slots[k])
        send(c2send.at[b], c2recv.at[b], ssem.at[C2, b], rsem.at[C2, b], partner)

    def c3(b):
        got(c2recv.at[b], rsem.at[C2, b])
        pieces = [c1recv[b, k] for k in range(KVH)]
        for k in range(4):
            x = pick(pieces, my_slots[k]).astype(F32) + c2recv[b, k].astype(F32)
            psum[b, k] = x.astype(BF16)
        c3recv[b, z] = psum[b, z]
        for d in (1, 3, 2):
            zz, dev = zpeer(d)
            send(psum.at[b, zz], c3recv.at[b, z], ssem.at[C3, b], rsem.at[C3, b], dev)

    def c4(b):
        got(c3recv.at[b, pl.ds(0, 3)], rsem.at[C3, b])
        attall[s, b] = jnp.sum(c3recv[b].astype(F32), axis=0).astype(BF16)
        for d in range(1, 8):
            piece = attall.at[s, b]
            send(piece, piece, ssem.at[C4, b], rsem.at[C4, b], {"seq": (s + d) % 8})

    def c5(b):
        got(c1recv.at[b, pl.ds(0, 7)], rsem.at[C4, b])

    for step, b in (
        (q1, 0), (q1, 1), (q1, 2), (q2, 0), (q1, 3), (q2, 1), (q1, 4), (q3, 0), (q2, 2), (q1, 5), (q3, 1), (q2, 3), (q4, 0),
    ):
        step(b)
    kv_load(0).wait()
    make_bias(0)
    qk(0, 0)

    def guarded(step, b):
        pl.when((b >= 0) & (b < NB))(lambda: step(b))

    def body(b, carry):
        for step, lead in ((q4, 1), (q3, 2), (q2, 4), (q1, 6)):
            guarded(step, b + lead)
        qk(b, 1)
        weigh(0)
        pv(jnp.maximum(b - 1, 0), 1)
        for step, lag in ((ml, 1), (c1, 3), (c2, 6), (c3, 7)):
            guarded(step, b - lag)
        after = jnp.minimum(b + 1, NB - 1)
        pl.when(b + 1 < NB)(lambda: kv_load(after).wait())
        make_bias(after)
        qk(after, 0)
        weigh(1)
        pv(b, 0)
        return carry

    lax.fori_loop(0, NB, body, 0)
    pv(NB - 1, 1)
    for step, b in (
        (ml, 7), (c1, 5), (c2, 2), (c3, 1), (c4, 0), (c1, 6), (c2, 3), (c3, 2), (c4, 1), (c1, 7), (c2, 4), (c3, 3), (c4, 2),
        (c2, 5), (c3, 4), (c4, 3), (c2, 6), (c3, 5), (c4, 4), (c2, 7), (c3, 6), (c4, 5), (c3, 7), (c4, 6), (c4, 7),
    ):
        step(b)
    for b in range(NB):
        c5(b)
    wload.wait()

    wide = w.shape[1] // NCH

    def project(n):
        x = jnp.concatenate([attall[j].reshape(ROWS, HD) for j in range(GS)], axis=1)
        y = jnp.dot(x, w[:, n * wide : (n + 1) * wide], preferred_element_type=F32).astype(BF16)
        for b in range(NB):
            ybuf[n, b % 2, b // 2] = y[b * QT : (b + 1) * QT]
        send(ybuf.at[n, other], d1recv.at[n], dssem.at[0, n], drsem.at[0, n], partner)

    def reduce_pair(n):
        got(d1recv.at[n], drsem.at[0, n])
        x = ybuf[n, c].astype(F32) + d1recv[n].astype(F32)
        d2send[n] = x.astype(BF16)
        d2recv[n, z] = d2send[n, z]
        for d in (1, 3, 2):
            zz, dev = zpeer(d)
            send(d2send.at[n, zz], d2recv.at[n, z], dssem.at[1, n], drsem.at[1, n], dev)

    def finish(n):
        got(d2recv.at[n, pl.ds(0, 3)], drsem.at[1, n])
        out_ref[0, :, n * wide : (n + 1) * wide] = jnp.sum(d2recv[n].astype(F32), axis=0).astype(BF16)

    project(0)
    project(1)
    reduce_pair(0)
    project(2)
    reduce_pair(1)
    project(3)
    reduce_pair(2)
    reduce_pair(3)

    def drain(b, carry):
        sent(q0recv.at[b], ssem.at[Q0, b])
        sent(q1recv.at[b, pl.ds(0, 3)], ssem.at[Q1, b])
        sent(q1recv.at[b, pl.ds(0, 3)], ssem.at[Q2, b])
        sent(qall.at[b, pl.ds(0, 4)], ssem.at[Q3, b])
        sent(mlrecv.at[b, pl.ds(0, 7)], ssem.at[ML, b])
        sent(c1recv.at[b, pl.ds(0, 7)], ssem.at[C1, b])
        sent(c2send.at[b], ssem.at[C2, b])
        sent(c3recv.at[b, pl.ds(0, 3)], ssem.at[C3, b])
        sent(c1recv.at[b, pl.ds(0, 7)], ssem.at[C4, b])
        return carry

    lax.fori_loop(0, NB, drain, 0)
    for n in range(NCH):
        sent(d1recv.at[n], dssem.at[0, n])
        sent(d2recv.at[n, pl.ds(0, 3)], dssem.at[1, n])
    for n in range(NCH):
        finish(n)


def local(query, cache, head_of_slot, lengths, out_weight):
    length = cache.shape[1]
    entries = cache.reshape(NB, length, 2 * HD)
    wide = out_weight.shape[1]
    vm = pltpu.VMEM
    dma = pltpu.SemaphoreType.DMA
    smem = pl.BlockSpec(memory_space=pltpu.SMEM)
    anywhere = pl.BlockSpec(memory_space=pl.ANY)
    return pl.pallas_call(
        kernel,
        out_shape=jax.ShapeDtypeStruct((1, QT, wide), BF16),
        in_specs=[smem, smem, anywhere, anywhere, anywhere],
        out_specs=pl.BlockSpec(memory_space=pltpu.VMEM),
        scratch_shapes=[
            vm((NB, QT, GS * HD), BF16),
            vm((NB, QT, 4 * HD), BF16),
            vm((NB, 4, QT, HD), BF16),
            vm((NB, 4, QT, HD), BF16),
            vm((NB, GS, QT, HD), BF16),
            vm((NB, length, 2 * HD), BF16),
            vm(out_weight.shape, BF16),
            vm((length, HD), BF16),
            vm((TILE, length), F32),
            vm((TILE, length), F32),
            vm((TILE, length), BF16),
            vm((TILE, length), BF16),
            vm((TILE, HD), F32),
            vm((TILE, HD), F32),
            vm((NB, ROWS, HD), F32),
            vm((NB, 8, HD), F32),
            vm((NB, 8, 8, HD), F32),
            vm((NB, GS, QT, HD), BF16),
            vm((NB, GS, QT, HD), BF16),
            vm((NB, 4, QT, HD), BF16),
            vm((NB, 4, QT, HD), BF16),
            vm((NB, 4, QT, HD), BF16),
            vm((NB, 4, QT, HD), BF16),
            vm((GS, NB, QT, HD), BF16),
            vm((NCH, 2, 4, QT, wide // NCH), BF16),
            vm((NCH, 4, QT, wide // NCH), BF16),
            vm((NCH, 4, QT, wide // NCH), BF16),
            vm((NCH, 4, QT, wide // NCH), BF16),
            dma((9, NB)),
            dma((9, NB)),
            dma((2, NCH)),
            dma((2, NCH)),
            dma((NB + 2,)),
        ],
        compiler_params=pltpu.CompilerParams(
            collective_id=0, has_side_effects=True, vmem_limit_bytes=58 * 2**20
        ),
        name="attend",
    )(head_of_slot, lengths, query, entries, out_weight)


def solution(mesh):
    in_specs = (
        P("grp", None, "tp"),
        P("grp", "tp", "seq", None),
        P("grp"),
        P("grp"),
        P("tp", "seq"),
    )
    out_specs = P(("grp", "tp"), None, "seq")
    return jax.shard_map(local, mesh=mesh, in_specs=in_specs, out_specs=out_specs, check_vma=False)
```

time: 368 us -> 75.9 us (0.21)
  waiting for transfers between devices: 201 us -> 0 us
  Pallas kernels: 0 us -> 74.2 us
  blocking collectives: 57.5 us -> 0 us
  other arithmetic: 42.7 us -> 0 us
  matrix products: 34.1 us -> 0 us
  between operations: 17.2 us -> 0.01 us
  local copies, waits for them, and re-layouts: 14.6 us -> 1.57 us
    all_gather x3 -> x0, waiting for transfers between devices: 200 us -> none  [the longest x2 140 us: from_root(): lax.all_gather(shard, axis)]
    pallas_call x0 -> x1, Pallas kernels: none -> 74.2 us  [local(): pl.pallas_call(kernel, out_shape=jax.ShapeDtypeStruct((1, QT, wide), BF16...]
    dot_general x9 -> x0, matrix products: 34.1 us -> none  [the longest x4 19.5 us: advance(): jnp.einsum('bnrk,bknd->bnrd', weights.astype(jnp.bfloat16), entry_block[....]
    all_to_all x1 -> x0, blocking collectives: 31.3 us -> none  [sum_at_owner(): lax.all_to_all(pieces, axis, split_axis=0, concat_axis=0, tiled=True)]
    add x23 -> x0, other arithmetic: 27.6 us -> none  [the longest x7 26.7 us: combine(): earlier[2] * early_scale[..., None] + latter[2] * late_scale[..., None]]
    all_gather x2 -> x0, blocking collectives: 26.2 us -> none  [merged(): everything = jax.tree.map(lambda part: lax.all_gather(part, axis), shard)]
    reduce_sum x6 -> x0, other arithmetic: 12.4 us -> none  [the longest x4 9.91 us: advance(): totals = totals * shrink + jnp.sum(weights, axis=3)]
    while x36 -> x0, local copies, waits for them, and re-layouts: 5.33 us -> none
  transfers between devices with their start and end apart: 3 -> 0, of which waited for: 3 -> 0; matrix products, arithmetic and copies ran while one was open for 1% -> 0% of each run, Pallas kernels for 0% -> 0%
where the time goes in v1:
time: 75.9 us; the launch traced here: 75.8 us
  Pallas kernels  74.2 us (98%)
  local copies, waits for them, and re-layouts  1.57 us (2%)
    pallas_call x1, Pallas kernels, local(): pl.pallas_call(kernel, out_shape=jax.ShapeDtypeStruct((1, QT, wide), BF16...  74.2 us
    unnamed x1, local copies, waits for them, and re-layouts  1.57 us

profile of v1, /device:TPU:1, one launch (start us, length us, event | category | flops | bytes accessed | tf_op | source)
XLA Modules:
  0.0 75.8 jit_solution(7505969955330825046)
XLA Ops:
  0.0 74.2 %attend.1 = bf16[1,64,1024]{2,1,0:T(8,128)(2,1)} custom-call(s32[8]{0:T(128)} %heads_ref.1, s32[8]{0:T(128)} %len_ref.1, bf16[8,64,1024]{2,1,0:T(8,128)(2,1)} %q_hbm.1, bf16[8,2048,256]{2,1,0:T(8,128)(2,1)} %bitcast.1, bf16[1024,1024]{1,0:T(8,128)(2,1)} %w_hbm.1), custom_call_target="tpu_custom_call" | custom-call | tf_op jit(solution)/shard_map/attend/pallas_call | solution.py:326
  74.2 1.6 %copy.7 = bf16[1,64,1024]{2,1,0:T(8,128)(2,1)} copy(bf16[1,64,1024]{2,1,0:T(8,128)(2,1)} %attend.1) | data formatting | bytes 262144

commit v2 on v1

v2 whole, which is shorter than its diff:
```python
import functools
import math

import jax
import jax.numpy as jnp
from jax import lax
from jax.experimental import pallas as pl
from jax.experimental.pallas import tpu as pltpu
from jax.sharding import PartitionSpec as P

HQ = 64
KVH = 8
HD = 128
NB = 8
QT = 64
GS = 8
ROWS = GS * QT
TILE = 256
MASKED = -1e30
EXP2_SCALE = math.log2(math.e) / math.sqrt(HD)
F32 = jnp.float32
BF16 = jnp.bfloat16
MESH = pl.DeviceIdType.MESH
Q0, Q1, Q2, Q3, C1, C1M, C3, C3M, C4 = range(9)


def kernel(
    heads_ref, len_ref, q_hbm, kv_hbm, w_hbm, out_ref,
    qown, q0recv, cand, q1recv, qall, kv, w, s0, s1, p0, p1, m0, m1,
    osend, mlbuf, c1recv, c1ml, c3send, c3sml, c3recv, c3ml, attall,
    ysend, yown, d1recv, d2send, d2recv, ssem, rsem, dssem, drsem, lsem,
):
    s = lax.axis_index("seq")
    t = lax.axis_index("tp")
    z = t // 2
    c = t % 2
    other = 1 - c
    length = kv.shape[1]
    head = heads_ref[s]
    head_chip = head // 2
    head_core = head % 2

    def slot_of(h):
        slot = jnp.int32(0)
        for k in range(KVH):
            slot = jnp.where(heads_ref[k] == h, k, slot)
        return slot

    slots = [slot_of(k) for k in range(KVH)]
    partner = {"tp": t + 1 - 2 * c}

    def zpeer(d):
        zz = (z + d) % 4
        return zz, {"tp": 2 * zz + c}

    def send(src, dst, ss, rs, dev):
        pltpu.make_async_remote_copy(
            src_ref=src, dst_ref=dst, send_sem=ss, recv_sem=rs, device_id=dev, device_id_type=MESH
        ).start()

    def got(ref, rs):
        pltpu.make_async_remote_copy(
            src_ref=ref, dst_ref=ref, send_sem=rs, recv_sem=rs, device_id=partner, device_id_type=MESH
        ).wait_recv()

    def sent(ref, ss):
        pltpu.make_async_remote_copy(
            src_ref=ref, dst_ref=ref, send_sem=ss, recv_sem=ss, device_id=partner, device_id_type=MESH
        ).wait_send()

    barrier = pltpu.get_barrier_semaphore()
    for d in range(1, 8):
        pl.semaphore_signal(barrier, inc=1, device_id={"tp": (t + d) % 8}, device_id_type=MESH)
        pl.semaphore_signal(barrier, inc=1, device_id={"seq": (s + d) % 8}, device_id_type=MESH)

    qload = pltpu.make_async_copy(q_hbm, qown, lsem.at[NB])
    qload.start()

    def kv_load(b):
        return pltpu.make_async_copy(kv_hbm.at[b], kv.at[b], lsem.at[b])

    wload = pltpu.make_async_copy(w_hbm, w, lsem.at[NB + 1])
    qload.wait()
    for b in range(NB):
        kv_load(b).start()
    wload.start()
    pl.semaphore_wait(barrier, 14)

    half = pl.multiple_of(c * 512, 512)
    other_half = pl.multiple_of(other * 512, 512)
    for b in range(NB):
        send(qown.at[b, :, pl.ds(other_half, 512)], q0recv.at[b], ssem.at[Q0, b], rsem.at[Q0, b], partner)

    def q1(b):
        got(q0recv.at[b], rsem.at[Q0, b])
        mine = qown[b, :, pl.ds(half, 512)]
        x = jnp.where(head_core == c, mine, q0recv[b])
        for k in range(4):
            cand[b, k] = x[:, k * HD : (k + 1) * HD]
        q1recv[b, z] = cand[b, z]
        for d in (2, 1, 3):
            zz, dev = zpeer(d)
            send(cand.at[b, zz], q1recv.at[b, z], ssem.at[Q1, b], rsem.at[Q1, b], dev)

    def q2(b):
        got(q1recv.at[b, pl.ds(0, 3)], rsem.at[Q1, b])
        qall[b, 4 * c + z] = pick([q1recv[b, k] for k in range(4)], head_chip)
        for d in (2, 1, 3):
            _, dev = zpeer(d)
            piece = qall.at[b, 4 * c + z]
            send(piece, piece, ssem.at[Q2, b], rsem.at[Q2, b], dev)

    def q3(b):
        got(q1recv.at[b, pl.ds(0, 3)], rsem.at[Q2, b])
        piece = qall.at[b, pl.ds(4 * c, 4)]
        send(piece, piece, ssem.at[Q3, b], rsem.at[Q3, b], partner)

    def q4(b):
        got(qall.at[b, pl.ds(4 * other, 4)], rsem.at[Q3, b])

    def pick(pieces, index):
        x = pieces[0]
        for k in range(1, len(pieces)):
            x = jnp.where(index == k, pieces[k], x)
        return x

    S, PR, M = (s0, s1), (p0, p1), (m0, m1)
    first = (4 * c, 4 * other)
    row_of = lax.broadcasted_iota(jnp.int32, (TILE, HD), 0)
    lane_of = lax.broadcasted_iota(jnp.int32, (TILE, HD), 1)
    hot = jnp.where(row_of % QT == lane_of, 1.0, 0.0).astype(BF16)
    ahead = (row_of[:HD] - lane_of[:HD]).astype(F32).astype(BF16)
    row, lane = row_of[:QT], lane_of[:QT]

    def bias(start, k):
        edge = jnp.clip(start - HD * k, -200, 200).astype(F32)
        edge = jnp.full((HD, HD), edge, F32).astype(BF16)
        return jnp.where(ahead > edge, jnp.asarray(MASKED, BF16), jnp.asarray(0, BF16))

    def qk(b, r):
        start = len_ref[b] - QT - t * length
        q = jnp.concatenate([qall[b, pl.ds(first[r], 4)].reshape(TILE, HD), hot], axis=1)
        top = None
        for k in range(length // 512):
            extra = jnp.concatenate([bias(start, 4 * k + i) for i in range(4)], axis=0)
            keys = jnp.concatenate([kv[b, k * 512 : (k + 1) * 512, :HD], extra], axis=1)
            x = lax.dot_general(q, keys, (((1,), (1,)), ((), ())), preferred_element_type=F32)
            S[r][:, k * 512 : (k + 1) * 512] = x
            for j in range(4):
                part = x[:, j * HD : (j + 1) * HD]
                top = part if top is None else jnp.maximum(top, part)
        M[r][...] = jnp.broadcast_to(jnp.max(top, axis=1, keepdims=True), (TILE, HD))

    def weigh(r):
        m = M[r][...]
        for k in range(length // HD):
            x = S[r][:, k * HD : (k + 1) * HD]
            PR[r][:, k * HD : (k + 1) * HD] = jnp.exp2((x - m) * EXP2_SCALE).astype(BF16)

    def pv(b, r):
        vals = jnp.concatenate([kv[b, :, HD:], jnp.ones((length, HD), BF16)], axis=1)
        acc = jnp.dot(PR[r][...], vals, preferred_element_type=F32)
        m = M[r][...]
        osend[b, pl.ds(first[r], 4)] = acc[:, :HD].astype(BF16).reshape(4, QT, HD)
        for j in range(4):
            rows = slice(j * QT, (j + 1) * QT)
            x = jnp.where(lane == row, m[rows], 0.0) + jnp.where(lane == row + QT, acc[rows, HD:], 0.0)
            mlbuf[b, first[r] + j] = jnp.sum(x, axis=0, keepdims=True)

    def to_rows(x):
        return jnp.sum(jnp.where(lane == row, jnp.broadcast_to(x, (QT, HD)), 0.0), axis=1, keepdims=True)

    def c1(b):
        c1recv[b, s] = osend[b, s]
        c1ml[b, s] = mlbuf[b, s]
        for d in (6, 2, 3, 5, 7, 1, 4):
            ss = (s + d) % 8
            send(osend.at[b, ss], c1recv.at[b, s], ssem.at[C1, b], rsem.at[C1, b], {"seq": ss})
            send(mlbuf.at[b, ss], c1ml.at[b, s], ssem.at[C1M, b], rsem.at[C1M, b], {"seq": ss})

    def c3(b):
        got(c1recv.at[b, pl.ds(0, 7)], rsem.at[C1, b])
        got(c1ml.at[b, pl.ds(0, 7)], rsem.at[C1M, b])
        pieces = [c1recv[b, k] for k in range(KVH)]
        rows = [c1ml[b, k] for k in range(KVH)]
        for k in range(KVH):
            c3send[b, k] = pick(pieces, slots[k])
            c3sml[b, k] = pick(rows, slots[k])
        c3recv[b, t] = c3send[b, t]
        c3ml[b, t] = c3sml[b, t]
        for d in (4, 5, 3, 2, 6, 7, 1):
            tt = (t + d) % 8
            send(c3send.at[b, tt], c3recv.at[b, t], ssem.at[C3, b], rsem.at[C3, b], {"tp": tt})
            send(c3sml.at[b, tt], c3ml.at[b, t], ssem.at[C3M, b], rsem.at[C3M, b], {"tp": tt})

    def c4(b):
        got(c3recv.at[b, pl.ds(0, 7)], rsem.at[C3, b])
        got(c3ml.at[b, pl.ds(0, 7)], rsem.at[C3M, b])
        ml = c3ml[b].reshape(8, HD)
        top = jnp.max(ml, axis=0, keepdims=True)
        scale = jnp.exp2((ml - top) * EXP2_SCALE)
        total = jnp.sum(ml * pltpu.roll(scale, QT, 1), axis=0, keepdims=True)
        scale = scale / pltpu.roll(jnp.broadcast_to(total, (8, HD)), QT, 1)
        x = c3recv[b, 0].astype(F32) * to_rows(scale[:1])
        for k in range(1, 8):
            x = x + c3recv[b, k].astype(F32) * to_rows(scale[k : k + 1])
        attall[b, s] = x.astype(BF16)
        for d in (6, 2, 3, 5, 7, 1, 4):
            piece = attall.at[b, s]
            send(piece, piece, ssem.at[C4, b], rsem.at[C4, b], {"seq": (s + d) % 8})

    def c5(b):
        got(c1recv.at[b, pl.ds(0, 7)], rsem.at[C4, b])
        x = jnp.concatenate([attall[b, j] for j in range(GS)], axis=1)
        y = jnp.dot(x, w[...], preferred_element_type=F32)

        @pl.when(c == b % 2)
        def _():
            yown[...] = y

        @pl.when(c != b % 2)
        def _():
            ysend[b // 2] = y.astype(BF16)
            send(ysend.at[b // 2], d1recv.at[b // 2], dssem.at[0, b // 2], drsem.at[0, b // 2], partner)

    def d2(b):
        k = b // 2

        @pl.when(c == b % 2)
        def _():
            got(d1recv.at[k], drsem.at[0, k])
            d2send[k] = (yown[...] + d1recv[k].astype(F32)).astype(BF16)

            @pl.when(z == k)
            def _():
                d2recv[k] = d2send[k]

            @pl.when(z != k)
            def _():
                send(d2send.at[k], d2recv.at[z], dssem.at[1, k], drsem.at[1, 0], {"tp": b})

    for step, b in (
        (q1, 0), (q1, 1), (q1, 2), (q2, 0), (q1, 3), (q2, 1), (q1, 4), (q3, 0), (q2, 2),
    ):
        step(b)
    kv_load(0).wait()
    qk(0, 0)

    def guarded(step, b):
        pl.when((b >= 0) & (b < NB))(lambda: step(b))

    def body(b, carry):
        for step, lead in ((q4, 0), (q3, 1), (q2, 3), (q1, 5), (c1, -1), (c3, -4), (c4, -7)):
            guarded(step, b + lead)
        after = jnp.minimum(b + 1, NB - 1)
        pl.when(b + 1 < NB)(lambda: kv_load(after).wait())
        qk(b, 1)
        weigh(0)
        pv(b, 0)
        weigh(1)
        qk(after, 0)
        pv(b, 1)
        return carry

    lax.fori_loop(0, NB, body, 0)
    c1(7)
    wload.wait()
    for step, b in (
        (c3, 4), (c4, 1), (c3, 5), (c4, 2), (c5, 0), (c3, 6), (c4, 3), (d2, 0), (c5, 1), (c3, 7), (c4, 4), (d2, 1), (c5, 2),
        (c4, 5), (d2, 2), (c5, 3), (c4, 6), (d2, 3), (c5, 4), (d2, 4), (c4, 7), (c5, 5), (d2, 5), (c5, 6), (d2, 6), (c5, 7), (d2, 7),
    ):
        step(b)
    got(d2recv.at[pl.ds(0, 3)], drsem.at[1, 0])
    out_ref[0] = jnp.sum(d2recv[...].astype(F32), axis=0).astype(BF16)

    def drain(b, carry):
        sent(q0recv.at[b], ssem.at[Q0, b])
        sent(q1recv.at[b, pl.ds(0, 3)], ssem.at[Q1, b])
        sent(q1recv.at[b, pl.ds(0, 3)], ssem.at[Q2, b])
        sent(qall.at[b, pl.ds(0, 4)], ssem.at[Q3, b])
        for k in (C1, C3, C4):
            sent(c1recv.at[b, pl.ds(0, 7)], ssem.at[k, b])
        for k in (C1M, C3M):
            sent(c1ml.at[b, pl.ds(0, 7)], ssem.at[k, b])
        return carry

    lax.fori_loop(0, NB, drain, 0)
    for k in range(4):
        sent(d1recv.at[k], dssem.at[0, k])
        pl.when(z != k)(lambda k=k: sent(d2send.at[k], dssem.at[1, k]))


def local(query, cache, head_of_slot, lengths, out_weight):
    length = cache.shape[1]
    entries = cache.reshape(NB, length, 2 * HD)
    wide = out_weight.shape[1]
    vm = pltpu.VMEM
    dma = pltpu.SemaphoreType.DMA
    smem = pl.BlockSpec(memory_space=pltpu.SMEM)
    anywhere = pl.BlockSpec(memory_space=pl.ANY)
    return pl.pallas_call(
        kernel,
        out_shape=jax.ShapeDtypeStruct((1, QT, wide), BF16),
        in_specs=[smem, smem, anywhere, anywhere, anywhere],
        out_specs=pl.BlockSpec(memory_space=pltpu.VMEM),
        scratch_shapes=[
            vm((NB, QT, GS * HD), BF16),
            vm((NB, QT, 4 * HD), BF16),
            vm((NB, 4, QT, HD), BF16),
            vm((NB, 4, QT, HD), BF16),
            vm((NB, GS, QT, HD), BF16),
            vm((NB, length, 2 * HD), BF16),
            vm(out_weight.shape, BF16),
            vm((TILE, length), F32),
            vm((TILE, length), F32),
            vm((TILE, length), BF16),
            vm((TILE, length), BF16),
            vm((TILE, HD), F32),
            vm((TILE, HD), F32),
            vm((NB, GS, QT, HD), BF16),
            vm((NB, GS, 1, HD), F32),
            vm((NB, KVH, QT, HD), BF16),
            vm((NB, KVH, 1, HD), F32),
            vm((NB, KVH, QT, HD), BF16),
            vm((NB, KVH, 1, HD), F32),
            vm((NB, 8, QT, HD), BF16),
            vm((NB, 8, 1, HD), F32),
            vm((NB, GS, QT, HD), BF16),
            vm((4, QT, wide), BF16),
            vm((QT, wide), F32),
            vm((4, QT, wide), BF16),
            vm((4, QT, wide), BF16),
            vm((4, QT, wide), BF16),
            dma((9, NB)),
            dma((9, NB)),
            dma((2, 4)),
            dma((2, 4)),
            dma((NB + 2,)),
        ],
        compiler_params=pltpu.CompilerParams(
            collective_id=0, has_side_effects=True, vmem_limit_bytes=58 * 2**20
        ),
        name="attend",
    )(head_of_slot, lengths, query, entries, out_weight)


def solution(mesh):
    in_specs = (
        P("grp", None, "tp"),
        P("grp", "tp", "seq", None),
        P("grp"),
        P("grp"),
        P("tp", "seq"),
    )
    out_specs = P(("grp", "tp"), None, "seq")
    return jax.shard_map(local, mesh=mesh, in_specs=in_specs, out_specs=out_specs, check_vma=False)
```

time: 75.9 us -> 61.3 us (0.81)
  Pallas kernels: 74.2 us -> 59.6 us
    pallas_call x1, Pallas kernels: 74.2 us -> 59.6 us  [local(): pl.pallas_call(kernel, out_shape=jax.ShapeDtypeStruct((1, QT, wide), BF16...]
where the time goes in v2:
time: 61.3 us; the launch traced here: 61.2 us
  Pallas kernels  59.6 us (97%)
  local copies, waits for them, and re-layouts  1.57 us (3%)
    pallas_call x1, Pallas kernels, local(): pl.pallas_call(kernel, out_shape=jax.ShapeDtypeStruct((1, QT, wide), BF16...  59.6 us
    unnamed x1, local copies, waits for them, and re-layouts  1.57 us

profile of v2, /device:TPU:1, one launch (start us, length us, event | category | flops | bytes accessed | tf_op | source)
XLA Modules:
  0.0 61.2 jit_solution(435033579567424892)
XLA Ops:
  0.0 59.6 %attend.1 = bf16[1,64,1024]{2,1,0:T(8,128)(2,1)} custom-call(s32[8]{0:T(128)} %heads_ref.1, s32[8]{0:T(128)} %len_ref.1, bf16[8,64,1024]{2,1,0:T(8,128)(2,1)} %q_hbm.1, bf16[8,2048,256]{2,1,0:T(8,128)(2,1)} %bitcast.1, bf16[1024,1024]{1,0:T(8,128)(2,1)} %w_hbm.1), custom_call_target="tpu_custom_call" | custom-call | tf_op jit(solution)/shard_map/attend/pallas_call | solution.py:301
  59.6 1.6 %copy.7 = bf16[1,64,1024]{2,1,0:T(8,128)(2,1)} copy(bf16[1,64,1024]{2,1,0:T(8,128)(2,1)} %attend.1) | data formatting | bytes 262144

commit v3 on v2

--- a/solution.py
+++ b/solution.py
@@ -240,7 +240,7 @@
                 send(d2send.at[k], d2recv.at[z], dssem.at[1, k], drsem.at[1, 0], {"tp": b})
 
     for step, b in (
-        (q1, 0), (q1, 1), (q1, 2), (q2, 0), (q1, 3), (q2, 1), (q1, 4), (q3, 0), (q2, 2),
+        (q1, 0), (q1, 1), (q2, 0), (q2, 1), (q1, 2), (q3, 0), (q1, 3), (q2, 2), (q1, 4),
     ):
         step(b)
     kv_load(0).wait()
@@ -266,8 +266,8 @@
     c1(7)
     wload.wait()
     for step, b in (
-        (c3, 4), (c4, 1), (c3, 5), (c4, 2), (c5, 0), (c3, 6), (c4, 3), (d2, 0), (c5, 1), (c3, 7), (c4, 4), (d2, 1), (c5, 2),
-        (c4, 5), (d2, 2), (c5, 3), (c4, 6), (d2, 3), (c5, 4), (d2, 4), (c4, 7), (c5, 5), (d2, 5), (c5, 6), (d2, 6), (c5, 7), (d2, 7),
+        (c3, 4), (c4, 1), (c4, 2), (c3, 5), (c4, 3), (c3, 6), (c5, 0), (c4, 4), (c3, 7), (d2, 0), (c5, 1), (c4, 5), (d2, 1), (c5, 2),
+        (d2, 2), (c4, 6), (c5, 3), (d2, 3), (c4, 7), (c5, 4), (d2, 4), (c5, 5), (d2, 5), (c5, 6), (d2, 6), (c5, 7), (d2, 7),
     ):
         step(b)
     got(d2recv.at[pl.ds(0, 3)], drsem.at[1, 0])
@@ -338,10 +338,10 @@
             dma((NB + 2,)),
         ],
         compiler_params=pltpu.CompilerParams(
-            collective_id=0, has_side_effects=True, vmem_limit_bytes=58 * 2**20
+            collective_id=0, has_side_effects=True, vmem_limit_bytes=40 * 2**20
         ),
         name="attend",
-    )(head_of_slot, lengths, query, entries, out_weight)
+    )(*[pltpu.with_memory_space_constraint(x, pltpu.HBM) for x in (head_of_slot, lengths, query, entries, out_weight)])
 
 
 def solution(mesh):

time: 61.3 us -> 62.5 us (1.020)
  Pallas kernels: 59.6 us -> 61.7 us
  local copies, waits for them, and re-layouts: 1.57 us -> 0.66 us
    pallas_call x1, Pallas kernels: 59.6 us -> 61.7 us  [local(): pl.pallas_call(kernel, out_shape=jax.ShapeDtypeStruct((1, QT, wide), BF16...]
    unnamed x1, local copies, waits for them, and re-layouts: 1.57 us -> 0.66 us
where the time goes in v3:
time: 62.5 us; the launch traced here: 62.3 us
  Pallas kernels  61.7 us (99%)
  local copies, waits for them, and re-layouts  0.66 us (1%)
    pallas_call x1, Pallas kernels, local(): pl.pallas_call(kernel, out_shape=jax.ShapeDtypeStruct((1, QT, wide), BF16...  61.7 us

profile of v3, /device:TPU:1, one launch (start us, length us, event | category | flops | bytes accessed | tf_op | source)
XLA Modules:
  0.0 62.3 jit_solution(16498595553506290416)
XLA Ops:
  0.0 61.7 %attend.1 = bf16[1,64,1024]{2,1,0:T(8,128)(2,1)S(1)} custom-call(s32[8]{0:T(128)} %heads_ref.1, s32[8]{0:T(128)} %len_ref.1, bf16[8,64,1024]{2,1,0:T(8,128)(2,1)} %q_hbm.1, bf16[8,2048,256]{2,1,0:T(8,128)(2,1)} %bitcast.1, bf16[1024,1024]{1,0:T(8,128)(2,1)} %w_hbm.1), custom_call_target="tpu_custom_call" | custom-call | tf_op jit(solution)/shard_map/attend/pallas_call | solution.py:301
  61.7 0.7 %copy.7 = bf16[1,64,1024]{2,1,0:T(8,128)(2,1)} copy(bf16[1,64,1024]{2,1,0:T(8,128)(2,1)S(1)} %attend.1) | data formatting | bytes 262144

commit v4 on v3

--- a/solution.py
+++ b/solution.py
@@ -216,7 +216,7 @@
 
         @pl.when(c == b % 2)
         def _():
-            yown[...] = y
+            yown[b // 2] = y
 
         @pl.when(c != b % 2)
         def _():
@@ -229,7 +229,7 @@
         @pl.when(c == b % 2)
         def _():
             got(d1recv.at[k], drsem.at[0, k])
-            d2send[k] = (yown[...] + d1recv[k].astype(F32)).astype(BF16)
+            d2send[k] = (yown[k] + d1recv[k].astype(F32)).astype(BF16)
 
             @pl.when(z == k)
             def _():
@@ -240,17 +240,18 @@
                 send(d2send.at[k], d2recv.at[z], dssem.at[1, k], drsem.at[1, 0], {"tp": b})
 
     for step, b in (
-        (q1, 0), (q1, 1), (q2, 0), (q2, 1), (q1, 2), (q3, 0), (q1, 3), (q2, 2), (q1, 4),
+        (q1, 0), (q1, 1), (q1, 2), (q1, 3), (q2, 0), (q1, 4), (q2, 1), (q1, 5), (q2, 2), (q2, 3), (q3, 0),
     ):
         step(b)
     kv_load(0).wait()
     qk(0, 0)
+    q3(1)
 
     def guarded(step, b):
         pl.when((b >= 0) & (b < NB))(lambda: step(b))
 
     def body(b, carry):
-        for step, lead in ((q4, 0), (q3, 1), (q2, 3), (q1, 5), (c1, -1), (c3, -4), (c4, -7)):
+        for step, lead in ((q4, 0), (c1, -1), (q3, 2), (q2, 4), (q1, 6), (c3, -4), (c4, -7)):
             guarded(step, b + lead)
         after = jnp.minimum(b + 1, NB - 1)
         pl.when(b + 1 < NB)(lambda: kv_load(after).wait())
@@ -266,8 +267,8 @@
     c1(7)
     wload.wait()
     for step, b in (
-        (c3, 4), (c4, 1), (c4, 2), (c3, 5), (c4, 3), (c3, 6), (c5, 0), (c4, 4), (c3, 7), (d2, 0), (c5, 1), (c4, 5), (d2, 1), (c5, 2),
-        (d2, 2), (c4, 6), (c5, 3), (d2, 3), (c4, 7), (c5, 4), (d2, 4), (c5, 5), (d2, 5), (c5, 6), (d2, 6), (c5, 7), (d2, 7),
+        (c3, 4), (c4, 1), (c4, 2), (c3, 5), (c4, 3), (c3, 6), (c5, 0), (c4, 4), (c5, 1), (c3, 7), (c4, 5), (c5, 2), (d2, 0),
+        (c4, 6), (d2, 1), (c5, 3), (c4, 7), (c5, 4), (d2, 2), (d2, 3), (c5, 5), (d2, 4), (c5, 6), (d2, 5), (c5, 7), (d2, 6), (d2, 7),
     ):
         step(b)
     got(d2recv.at[pl.ds(0, 3)], drsem.at[1, 0])
@@ -327,7 +328,7 @@
             vm((NB, 8, 1, HD), F32),
             vm((NB, GS, QT, HD), BF16),
             vm((4, QT, wide), BF16),
-            vm((QT, wide), F32),
+            vm((4, QT, wide), F32),
             vm((4, QT, wide), BF16),
             vm((4, QT, wide), BF16),
             vm((4, QT, wide), BF16),

time: 62.5 us -> 59.6 us (0.954)
  Pallas kernels: 61.7 us -> 58.8 us
    pallas_call x1, Pallas kernels: 61.7 us -> 58.8 us  [local(): pl.pallas_call(kernel, out_shape=jax.ShapeDtypeStruct((1, QT, wide), BF16...]
where the time goes in v4:
time: 59.6 us; the launch traced here: 59.4 us
  Pallas kernels  58.8 us (99%)
  local copies, waits for them, and re-layouts  0.66 us (1%)
    pallas_call x1, Pallas kernels, local(): pl.pallas_call(kernel, out_shape=jax.ShapeDtypeStruct((1, QT, wide), BF16...  58.8 us

profile of v4, /device:TPU:1, one launch (start us, length us, event | category | flops | bytes accessed | tf_op | source)
XLA Modules:
  0.0 59.4 jit_solution(4614493719077813148)
XLA Ops:
  0.0 58.8 %attend.1 = bf16[1,64,1024]{2,1,0:T(8,128)(2,1)S(1)} custom-call(s32[8]{0:T(128)} %heads_ref.1, s32[8]{0:T(128)} %len_ref.1, bf16[8,64,1024]{2,1,0:T(8,128)(2,1)} %q_hbm.1, bf16[8,2048,256]{2,1,0:T(8,128)(2,1)} %bitcast.1, bf16[1024,1024]{1,0:T(8,128)(2,1)} %w_hbm.1), custom_call_target="tpu_custom_call" | custom-call | tf_op jit(solution)/shard_map/attend/pallas_call | solution.py:302
  58.8 0.7 %copy.7 = bf16[1,64,1024]{2,1,0:T(8,128)(2,1)} copy(bf16[1,64,1024]{2,1,0:T(8,128)(2,1)S(1)} %attend.1) | data formatting | bytes 262144

commit v5 on v4

--- a/solution.py
+++ b/solution.py
@@ -22,6 +22,10 @@
 BF16 = jnp.bfloat16
 MESH = pl.DeviceIdType.MESH
 Q0, Q1, Q2, Q3, C1, C1M, C3, C3M, C4 = range(9)
+
+
+def sequence(i):
+    return 2 * ((i + 3) % 4) + (i + i // 4 + 1) % 2
 
 
 def kernel(
@@ -77,7 +81,7 @@
     qload.start()
 
     def kv_load(b):
-        return pltpu.make_async_copy(kv_hbm.at[b], kv.at[b], lsem.at[b])
+        return pltpu.make_async_copy(kv_hbm.at[sequence(b)], kv.at[b], lsem.at[b])
 
     wload = pltpu.make_async_copy(w_hbm, w, lsem.at[NB + 1])
     qload.wait()
@@ -89,11 +93,11 @@
     half = pl.multiple_of(c * 512, 512)
     other_half = pl.multiple_of(other * 512, 512)
     for b in range(NB):
-        send(qown.at[b, :, pl.ds(other_half, 512)], q0recv.at[b], ssem.at[Q0, b], rsem.at[Q0, b], partner)
+        send(qown.at[sequence(b), :, pl.ds(other_half, 512)], q0recv.at[b], ssem.at[Q0, b], rsem.at[Q0, b], partner)
 
     def q1(b):
         got(q0recv.at[b], rsem.at[Q0, b])
-        mine = qown[b, :, pl.ds(half, 512)]
+        mine = qown[sequence(b), :, pl.ds(half, 512)]
         x = jnp.where(head_core == c, mine, q0recv[b])
         for k in range(4):
             cand[b, k] = x[:, k * HD : (k + 1) * HD]
@@ -138,7 +142,7 @@
         return jnp.where(ahead > edge, jnp.asarray(MASKED, BF16), jnp.asarray(0, BF16))
 
     def qk(b, r):
-        start = len_ref[b] - QT - t * length
+        start = len_ref[sequence(b)] - QT - t * length
         q = jnp.concatenate([qall[b, pl.ds(first[r], 4)].reshape(TILE, HD), hot], axis=1)
         top = None
         for k in range(length // 512):
@@ -214,19 +218,21 @@
         x = jnp.concatenate([attall[b, j] for j in range(GS)], axis=1)
         y = jnp.dot(x, w[...], preferred_element_type=F32)
 
-        @pl.when(c == b % 2)
+        k, core = divmod(sequence(b), 2)
+
+        @pl.when(c == core)
         def _():
-            yown[b // 2] = y
-
-        @pl.when(c != b % 2)
+            yown[k] = y
+
+        @pl.when(c != core)
         def _():
-            ysend[b // 2] = y.astype(BF16)
-            send(ysend.at[b // 2], d1recv.at[b // 2], dssem.at[0, b // 2], drsem.at[0, b // 2], partner)
+            ysend[k] = y.astype(BF16)
+            send(ysend.at[k], d1recv.at[k], dssem.at[0, k], drsem.at[0, k], partner)
 
     def d2(b):
-        k = b // 2
-
-        @pl.when(c == b % 2)
+        k, core = divmod(sequence(b), 2)
+
+        @pl.when(c == core)
         def _():
             got(d1recv.at[k], drsem.at[0, k])
             d2send[k] = (yown[k] + d1recv[k].astype(F32)).astype(BF16)
@@ -237,21 +243,21 @@
 
             @pl.when(z != k)
             def _():
-                send(d2send.at[k], d2recv.at[z], dssem.at[1, k], drsem.at[1, 0], {"tp": b})
+                send(d2send.at[k], d2recv.at[z], dssem.at[1, k], drsem.at[1, 0], {"tp": sequence(b)})
 
     for step, b in (
-        (q1, 0), (q1, 1), (q1, 2), (q1, 3), (q2, 0), (q1, 4), (q2, 1), (q1, 5), (q2, 2), (q2, 3), (q3, 0),
+        (q1, 0), (q1, 1), (q1, 2), (q1, 3), (q2, 0), (q2, 1), (q1, 4), (q2, 2), (q1, 5), (q3, 0),
     ):
         step(b)
     kv_load(0).wait()
     qk(0, 0)
-    q3(1)
+    q2(3)
 
     def guarded(step, b):
         pl.when((b >= 0) & (b < NB))(lambda: step(b))
 
     def body(b, carry):
-        for step, lead in ((q4, 0), (c1, -1), (q3, 2), (q2, 4), (q1, 6), (c3, -4), (c4, -7)):
+        for step, lead in ((q4, 0), (c1, -1), (q3, 1), (q2, 4), (q1, 6), (c3, -4), (c4, -7)):
             guarded(step, b + lead)
         after = jnp.minimum(b + 1, NB - 1)
         pl.when(b + 1 < NB)(lambda: kv_load(after).wait())
@@ -267,8 +273,8 @@
     c1(7)
     wload.wait()
     for step, b in (
-        (c3, 4), (c4, 1), (c4, 2), (c3, 5), (c4, 3), (c3, 6), (c5, 0), (c4, 4), (c5, 1), (c3, 7), (c4, 5), (c5, 2), (d2, 0),
-        (c4, 6), (d2, 1), (c5, 3), (c4, 7), (c5, 4), (d2, 2), (d2, 3), (c5, 5), (d2, 4), (c5, 6), (d2, 5), (c5, 7), (d2, 6), (d2, 7),
+        (c3, 4), (c4, 1), (c4, 2), (c3, 5), (c3, 6), (c4, 3), (c3, 7), (c5, 0), (c4, 4), (c5, 1), (c4, 5), (c5, 2), (c4, 6),
+        (d2, 0), (c5, 3), (d2, 1), (c4, 7), (c5, 4), (d2, 2), (c5, 5), (d2, 3), (c5, 6), (d2, 4), (d2, 5), (c5, 7), (d2, 6), (d2, 7),
     ):
         step(b)
     got(d2recv.at[pl.ds(0, 3)], drsem.at[1, 0])

time: 59.6 us -> 55.2 us (0.926)
  Pallas kernels: 58.8 us -> 54.4 us
    pallas_call x1, Pallas kernels: 58.8 us -> 54.4 us  [local(): pl.pallas_call(kernel, out_shape=jax.ShapeDtypeStruct((1, QT, wide), BF16...]
where the time goes in v5:
time: 55.2 us; the launch traced here: 55 us
  Pallas kernels  54.4 us (99%)
  local copies, waits for them, and re-layouts  0.66 us (1%)
    pallas_call x1, Pallas kernels, local(): pl.pallas_call(kernel, out_shape=jax.ShapeDtypeStruct((1, QT, wide), BF16...  54.4 us

profile of v5, /device:TPU:1, one launch (start us, length us, event | category | flops | bytes accessed | tf_op | source)
XLA Modules:
  0.0 55.0 jit_solution(1196358232302119050)
XLA Ops:
  0.0 54.4 %attend.1 = bf16[1,64,1024]{2,1,0:T(8,128)(2,1)S(1)} custom-call(s32[8]{0:T(128)} %heads_ref.1, s32[8]{0:T(128)} %len_ref.1, bf16[8,64,1024]{2,1,0:T(8,128)(2,1)} %q_hbm.1, bf16[8,2048,256]{2,1,0:T(8,128)(2,1)} %bitcast.1, bf16[1024,1024]{1,0:T(8,128)(2,1)} %w_hbm.1), custom_call_target="tpu_custom_call" | custom-call | tf_op jit(solution)/shard_map/attend/pallas_call | solution.py:308
  54.4 0.7 %copy.7 = bf16[1,64,1024]{2,1,0:T(8,128)(2,1)} copy(bf16[1,64,1024]{2,1,0:T(8,128)(2,1)S(1)} %attend.1) | data formatting | bytes 262144

commit v6 on v5

--- a/solution.py
+++ b/solution.py
@@ -29,8 +29,8 @@
 
 
 def kernel(
-    heads_ref, len_ref, q_hbm, kv_hbm, w_hbm, out_ref,
-    qown, q0recv, cand, q1recv, qall, kv, w, s0, s1, p0, p1, m0, m1,
+    heads_hbm, len_hbm, q_hbm, kv_hbm, w_hbm, out_ref,
+    heads_ref, len_ref, qown, q0recv, cand, q1recv, qall, kv, w, s0, s1, p0, p1, m0, m1,
     osend, mlbuf, c1recv, c1ml, c3send, c3sml, c3recv, c3ml, attall,
     ysend, yown, d1recv, d2send, d2recv, ssem, rsem, dssem, drsem, lsem,
 ):
@@ -40,6 +40,45 @@
     c = t % 2
     other = 1 - c
     length = kv.shape[1]
+    partner = {"tp": t + 1 - 2 * c}
+
+    def zpeer(d):
+        zz = (z + d) % 4
+        return zz, {"tp": 2 * zz + c}
+
+    def send(src, dst, ss, rs, dev):
+        pltpu.make_async_remote_copy(
+            src_ref=src, dst_ref=dst, send_sem=ss, recv_sem=rs, device_id=dev, device_id_type=MESH
+        ).start()
+
+    def got(ref, rs):
+        pltpu.make_async_remote_copy(
+            src_ref=ref, dst_ref=ref, send_sem=rs, recv_sem=rs, device_id=partner, device_id_type=MESH
+        ).wait_recv()
+
+    def sent(ref, ss):
+        pltpu.make_async_remote_copy(
+            src_ref=ref, dst_ref=ref, send_sem=ss, recv_sem=ss, device_id=partner, device_id_type=MESH
+        ).wait_send()
+
+    barrier = pltpu.get_barrier_semaphore()
+    for d in range(1, 8):
+        pl.semaphore_signal(barrier, inc=1, device_id={"tp": (t + d) % 8}, device_id_type=MESH)
+        pl.semaphore_signal(barrier, inc=1, device_id={"seq": (s + d) % 8}, device_id_type=MESH)
+
+    qload = pltpu.make_async_copy(q_hbm, qown, lsem.at[NB])
+    qload.start()
+
+    def kv_load(b):
+        return pltpu.make_async_copy(kv_hbm.at[sequence(b)], kv.at[b], lsem.at[b])
+
+    wload = pltpu.make_async_copy(w_hbm, w, lsem.at[NB + 1])
+    heads_load = pltpu.make_async_copy(heads_hbm, heads_ref, lsem.at[NB + 2])
+    len_load = pltpu.make_async_copy(len_hbm, len_ref, lsem.at[NB + 3])
+    heads_load.start()
+    len_load.start()
+    heads_load.wait()
+    len_load.wait()
     head = heads_ref[s]
     head_chip = head // 2
     head_core = head % 2
@@ -51,39 +90,6 @@
         return slot
 
     slots = [slot_of(k) for k in range(KVH)]
-    partner = {"tp": t + 1 - 2 * c}
-
-    def zpeer(d):
-        zz = (z + d) % 4
-        return zz, {"tp": 2 * zz + c}
-
-    def send(src, dst, ss, rs, dev):
-        pltpu.make_async_remote_copy(
-            src_ref=src, dst_ref=dst, send_sem=ss, recv_sem=rs, device_id=dev, device_id_type=MESH
-        ).start()
-
-    def got(ref, rs):
-        pltpu.make_async_remote_copy(
-            src_ref=ref, dst_ref=ref, send_sem=rs, recv_sem=rs, device_id=partner, device_id_type=MESH
-        ).wait_recv()
-
-    def sent(ref, ss):
-        pltpu.make_async_remote_copy(
-            src_ref=ref, dst_ref=ref, send_sem=ss, recv_sem=ss, device_id=partner, device_id_type=MESH
-        ).wait_send()
-
-    barrier = pltpu.get_barrier_semaphore()
-    for d in range(1, 8):
-        pl.semaphore_signal(barrier, inc=1, device_id={"tp": (t + d) % 8}, device_id_type=MESH)
-        pl.semaphore_signal(barrier, inc=1, device_id={"seq": (s + d) % 8}, device_id_type=MESH)
-
-    qload = pltpu.make_async_copy(q_hbm, qown, lsem.at[NB])
-    qload.start()
-
-    def kv_load(b):
-        return pltpu.make_async_copy(kv_hbm.at[sequence(b)], kv.at[b], lsem.at[b])
-
-    wload = pltpu.make_async_copy(w_hbm, w, lsem.at[NB + 1])
     qload.wait()
     for b in range(NB):
         kv_load(b).start()
@@ -92,7 +98,7 @@
 
     half = pl.multiple_of(c * 512, 512)
     other_half = pl.multiple_of(other * 512, 512)
-    for b in range(NB):
+    def q0(b):
         send(qown.at[sequence(b), :, pl.ds(other_half, 512)], q0recv.at[b], ssem.at[Q0, b], rsem.at[Q0, b], partner)
 
     def q1(b):
@@ -245,36 +251,58 @@
             def _():
                 send(d2send.at[k], d2recv.at[z], dssem.at[1, k], drsem.at[1, 0], {"tp": sequence(b)})
 
-    for step, b in (
-        (q1, 0), (q1, 1), (q1, 2), (q1, 3), (q2, 0), (q2, 1), (q1, 4), (q2, 2), (q1, 5), (q3, 0),
-    ):
-        step(b)
+    q0(0)
+    q1(0)
+    for b in range(1, 4):
+        q0(b)
+    q1(1)
+    q1(2)
+    for b in range(4, NB):
+        q0(b)
+    q1(3)
+    q2(0)
+    q2(1)
+    q1(4)
+    q2(2)
+    q1(5)
+    q3(0)
     kv_load(0).wait()
     qk(0, 0)
-    q2(3)
 
     def guarded(step, b):
         pl.when((b >= 0) & (b < NB))(lambda: step(b))
 
+    def steps_at(b):
+        for step, lead in ((q4, 0), (c1, -1), (q3, 1), (q2, 3), (q1, 6), (c3, -4), (c4, -7)):
+            if not isinstance(b, int):
+                if step is not c4:
+                    guarded(step, b + lead)
+            elif 0 <= b + lead < NB:
+                step(b + lead)
+
     def body(b, carry):
-        for step, lead in ((q4, 0), (c1, -1), (q3, 1), (q2, 4), (q1, 6), (c3, -4), (c4, -7)):
-            guarded(step, b + lead)
-        after = jnp.minimum(b + 1, NB - 1)
-        pl.when(b + 1 < NB)(lambda: kv_load(after).wait())
+        steps_at(b)
+        kv_load(b + 1).wait()
         qk(b, 1)
         weigh(0)
         pv(b, 0)
         weigh(1)
-        qk(after, 0)
+        qk(b + 1, 0)
         pv(b, 1)
         return carry
 
-    lax.fori_loop(0, NB, body, 0)
-    c1(7)
+    lax.fori_loop(0, NB - 1, body, 0)
+    last = NB - 1
+    steps_at(last)
+    qk(last, 1)
+    weigh(0)
+    pv(last, 0)
+    weigh(1)
+    pv(last, 1)
+    c1(last)
     wload.wait()
     for step, b in (
-        (c3, 4), (c4, 1), (c4, 2), (c3, 5), (c3, 6), (c4, 3), (c3, 7), (c5, 0), (c4, 4), (c5, 1), (c4, 5), (c5, 2), (c4, 6),
-        (d2, 0), (c5, 3), (d2, 1), (c4, 7), (c5, 4), (d2, 2), (c5, 5), (d2, 3), (c5, 6), (d2, 4), (d2, 5), (c5, 7), (d2, 6), (d2, 7),
+        (c3, 4), (c3, 5), (c4, 1), (c4, 2), (c3, 6), (c4, 3), (c3, 7), (c5, 0), (c4, 4), (c5, 1), (c4, 5), (c5, 2), (c4, 6), (d2, 0), (c5, 3), (d2, 1), (c4, 7), (c5, 4), (d2, 2), (c5, 5), (d2, 3), (c5, 6), (d2, 4), (d2, 5), (c5, 7), (d2, 6), (d2, 7),
     ):
         step(b)
     got(d2recv.at[pl.ds(0, 3)], drsem.at[1, 0])
@@ -303,14 +331,15 @@
     wide = out_weight.shape[1]
     vm = pltpu.VMEM
     dma = pltpu.SemaphoreType.DMA
-    smem = pl.BlockSpec(memory_space=pltpu.SMEM)
     anywhere = pl.BlockSpec(memory_space=pl.ANY)
     return pl.pallas_call(
         kernel,
         out_shape=jax.ShapeDtypeStruct((1, QT, wide), BF16),
-        in_specs=[smem, smem, anywhere, anywhere, anywhere],
+        in_specs=[anywhere] * 5,
         out_specs=pl.BlockSpec(memory_space=pltpu.VMEM),
         scratch_shapes=[
+            pltpu.SMEM((KVH,), jnp.int32),
+            pltpu.SMEM((NB,), jnp.int32),
             vm((NB, QT, GS * HD), BF16),
             vm((NB, QT, 4 * HD), BF16),
             vm((NB, 4, QT, HD), BF16),
@@ -342,7 +371,7 @@
             dma((9, NB)),
             dma((2, 4)),
             dma((2, 4)),
-            dma((NB + 2,)),
+            dma((NB + 4,)),
         ],
         compiler_params=pltpu.CompilerParams(
             collective_id=0, has_side_effects=True, vmem_limit_bytes=40 * 2**20

time: 55.2 us -> 53.6 us (0.971)
  Pallas kernels: 54.4 us -> 52.8 us
    pallas_call x1, Pallas kernels: 54.4 us -> 52.8 us  [local(): pl.pallas_call(kernel, out_shape=jax.ShapeDtypeStruct((1, QT, wide), BF16...]
where the time goes in v6:
time: 53.6 us; the launch traced here: 53.5 us
  Pallas kernels  52.8 us (99%)
  local copies, waits for them, and re-layouts  0.66 us (1%)
    pallas_call x1, Pallas kernels, local(): pl.pallas_call(kernel, out_shape=jax.ShapeDtypeStruct((1, QT, wide), BF16...  52.8 us

profile of v6, /device:TPU:1, one launch (start us, length us, event | category | flops | bytes accessed | tf_op | source)
XLA Modules:
  0.0 53.5 jit_solution(6287096526503077991)
XLA Ops:
  0.0 52.8 %attend.1 = bf16[1,64,1024]{2,1,0:T(8,128)(2,1)S(1)} custom-call(s32[8]{0:T(128)} %heads_hbm.1, s32[8]{0:T(128)} %len_hbm.1, bf16[8,64,1024]{2,1,0:T(8,128)(2,1)} %q_hbm.1, bf16[8,2048,256]{2,1,0:T(8,128)(2,1)} %bitcast.1, bf16[1024,1024]{1,0:T(8,128)(2,1)} %w_hbm.1), custom_call_target="tpu_custom_call" | custom-call | tf_op jit(solution)/shard_map/attend/pallas_call | solution.py:335
  52.8 0.7 %copy.7 = bf16[1,64,1024]{2,1,0:T(8,128)(2,1)} copy(bf16[1,64,1024]{2,1,0:T(8,128)(2,1)S(1)} %attend.1) | data formatting | bytes 262144

commit v7 on v6

--- a/solution.py
+++ b/solution.py
@@ -177,16 +177,15 @@
             x = jnp.where(lane == row, m[rows], 0.0) + jnp.where(lane == row + QT, acc[rows, HD:], 0.0)
             mlbuf[b, first[r] + j] = jnp.sum(x, axis=0, keepdims=True)
 
-    def to_rows(x):
-        return jnp.sum(jnp.where(lane == row, jnp.broadcast_to(x, (QT, HD)), 0.0), axis=1, keepdims=True)
-
     def c1(b):
         c1recv[b, s] = osend[b, s]
         c1ml[b, s] = mlbuf[b, s]
         for d in (6, 2, 3, 5, 7, 1, 4):
             ss = (s + d) % 8
+            send(mlbuf.at[b, ss], c1ml.at[b, s], ssem.at[C1M, b], rsem.at[C1M, b], {"seq": ss})
+        for d in (6, 2, 3, 5, 7, 1, 4):
+            ss = (s + d) % 8
             send(osend.at[b, ss], c1recv.at[b, s], ssem.at[C1, b], rsem.at[C1, b], {"seq": ss})
-            send(mlbuf.at[b, ss], c1ml.at[b, s], ssem.at[C1M, b], rsem.at[C1M, b], {"seq": ss})
 
     def c3(b):
         got(c1recv.at[b, pl.ds(0, 7)], rsem.at[C1, b])
@@ -200,8 +199,10 @@
         c3ml[b, t] = c3sml[b, t]
         for d in (4, 5, 3, 2, 6, 7, 1):
             tt = (t + d) % 8
+            send(c3sml.at[b, tt], c3ml.at[b, t], ssem.at[C3M, b], rsem.at[C3M, b], {"tp": tt})
+        for d in (4, 5, 3, 2, 6, 7, 1):
+            tt = (t + d) % 8
             send(c3send.at[b, tt], c3recv.at[b, t], ssem.at[C3, b], rsem.at[C3, b], {"tp": tt})
-            send(c3sml.at[b, tt], c3ml.at[b, t], ssem.at[C3M, b], rsem.at[C3M, b], {"tp": tt})
 
     def c4(b):
         got(c3recv.at[b, pl.ds(0, 7)], rsem.at[C3, b])
@@ -211,9 +212,10 @@
         scale = jnp.exp2((ml - top) * EXP2_SCALE)
         total = jnp.sum(ml * pltpu.roll(scale, QT, 1), axis=0, keepdims=True)
         scale = scale / pltpu.roll(jnp.broadcast_to(total, (8, HD)), QT, 1)
-        x = c3recv[b, 0].astype(F32) * to_rows(scale[:1])
+        columns = jnp.transpose(scale)[:QT]
+        x = c3recv[b, 0].astype(F32) * columns[:, :1]
         for k in range(1, 8):
-            x = x + c3recv[b, k].astype(F32) * to_rows(scale[k : k + 1])
+            x = x + c3recv[b, k].astype(F32) * columns[:, k : k + 1]
         attall[b, s] = x.astype(BF16)
         for d in (6, 2, 3, 5, 7, 1, 4):
             piece = attall.at[b, s]

time: 53.6 us -> 53.6 us (level)
  no operation moved by 1% of the time
where the time goes in v7:
time: 53.6 us; the launch traced here: 53.5 us
  Pallas kernels  52.8 us (99%)
  local copies, waits for them, and re-layouts  0.66 us (1%)
    pallas_call x1, Pallas kernels, local(): pl.pallas_call(kernel, out_shape=jax.ShapeDtypeStruct((1, QT, wide), BF16...  52.8 us

profile of v7, /device:TPU:1, one launch (start us, length us, event | category | flops | bytes accessed | tf_op | source)
XLA Modules:
  0.0 53.5 jit_solution(16651243207032712938)
XLA Ops:
  0.0 52.8 %attend.1 = bf16[1,64,1024]{2,1,0:T(8,128)(2,1)S(1)} custom-call(s32[8]{0:T(128)} %heads_hbm.1, s32[8]{0:T(128)} %len_hbm.1, bf16[8,64,1024]{2,1,0:T(8,128)(2,1)} %q_hbm.1, bf16[8,2048,256]{2,1,0:T(8,128)(2,1)} %bitcast.1, bf16[1024,1024]{1,0:T(8,128)(2,1)} %w_hbm.1), custom_call_target="tpu_custom_call" | custom-call | tf_op jit(solution)/shard_map/attend/pallas_call | solution.py:337
  52.8 0.7 %copy.7 = bf16[1,64,1024]{2,1,0:T(8,128)(2,1)} copy(bf16[1,64,1024]{2,1,0:T(8,128)(2,1)S(1)} %attend.1) | data formatting | bytes 262144

commit v8 on v6

--- a/solution.py
+++ b/solution.py
@@ -66,8 +66,11 @@
         pl.semaphore_signal(barrier, inc=1, device_id={"tp": (t + d) % 8}, device_id_type=MESH)
         pl.semaphore_signal(barrier, inc=1, device_id={"seq": (s + d) % 8}, device_id_type=MESH)
 
-    qload = pltpu.make_async_copy(q_hbm, qown, lsem.at[NB])
-    qload.start()
+    def q_load(b):
+        return pltpu.make_async_copy(q_hbm.at[sequence(b)], qown.at[sequence(b)], lsem.at[NB + 4 + b])
+
+    for b in range(NB):
+        q_load(b).start()
 
     def kv_load(b):
         return pltpu.make_async_copy(kv_hbm.at[sequence(b)], kv.at[b], lsem.at[b])
@@ -90,7 +93,7 @@
         return slot
 
     slots = [slot_of(k) for k in range(KVH)]
-    qload.wait()
+    q_load(0).wait()
     for b in range(NB):
         kv_load(b).start()
     wload.start()
@@ -99,6 +102,8 @@
     half = pl.multiple_of(c * 512, 512)
     other_half = pl.multiple_of(other * 512, 512)
     def q0(b):
+        if b:
+            q_load(b).wait()
         send(qown.at[sequence(b), :, pl.ds(other_half, 512)], q0recv.at[b], ssem.at[Q0, b], rsem.at[Q0, b], partner)
 
     def q1(b):
@@ -371,7 +376,7 @@
             dma((9, NB)),
             dma((2, 4)),
             dma((2, 4)),
-            dma((NB + 4,)),
+            dma((2 * NB + 4,)),
         ],
         compiler_params=pltpu.CompilerParams(
             collective_id=0, has_side_effects=True, vmem_limit_bytes=40 * 2**20

time: 53.6 us -> 53.7 us (level)
  no operation moved by 1% of the time
where the time goes in v8:
time: 53.7 us; the launch traced here: 53.5 us
  Pallas kernels  52.9 us (99%)
  local copies, waits for them, and re-layouts  0.66 us (1%)
    pallas_call x1, Pallas kernels, local(): pl.pallas_call(kernel, out_shape=jax.ShapeDtypeStruct((1, QT, wide), BF16...  52.9 us

profile of v8, /device:TPU:1, one launch (start us, length us, event | category | flops | bytes accessed | tf_op | source)
XLA Modules:
  0.0 53.5 jit_solution(9030566075185812822)
XLA Ops:
  0.0 52.9 %attend.1 = bf16[1,64,1024]{2,1,0:T(8,128)(2,1)S(1)} custom-call(s32[8]{0:T(128)} %heads_hbm.1, s32[8]{0:T(128)} %len_hbm.1, bf16[8,64,1024]{2,1,0:T(8,128)(2,1)} %q_hbm.1, bf16[8,2048,256]{2,1,0:T(8,128)(2,1)} %bitcast.1, bf16[1024,1024]{1,0:T(8,128)(2,1)} %w_hbm.1), custom_call_target="tpu_custom_call" | custom-call | tf_op jit(solution)/shard_map/attend/pallas_call | solution.py:340
  52.9 0.7 %copy.7 = bf16[1,64,1024]{2,1,0:T(8,128)(2,1)} copy(bf16[1,64,1024]{2,1,0:T(8,128)(2,1)S(1)} %attend.1) | data formatting | bytes 262144
